TPU v7x, 32 devices: a whole 2x2x4 slice. The times are simulated.
32 devices in a mesh: fsdp: 8 (over z, y), dp: 4 (over x, core).
Axes of the slice: x: 2, y: 2, z: 4, core: 2. Of those that a mesh axis runs over, the one named last changes fastest.
Arguments:
- tokens: bfloat16 [512, 4096], P('dp', 'fsdp'), may hold values from -6 to 6
- out_grad: bfloat16 [512, 5120], P('dp', 'fsdp'), may hold values from -0.26367188 to 0.26367188
- master: float32 [4096, 5120], P('fsdp'), may hold values from -0.09375 to 0.09375
- moment_one: float32 [4096, 5120], P('fsdp'), may hold values from -3 to 3
- moment_two: float32 [4096, 5120], P('fsdp'), may hold values from 0.1 to 4
- flags: int32 [32, 16], P(('fsdp', 'dp')), may hold values 0 or 1
- steps: int32 [16], replicated, may hold values from 1 to 8
- rate: float32 [1], replicated, may hold values from 0.001 to 0.01
Outputs:
- master_next: float32 [4096, 5120], P('fsdp')
- moment_one_next: float32 [4096, 5120], P('fsdp')
- moment_two_next: float32 [4096, 5120], P('fsdp')
- weight_half: bfloat16 [4096, 5120], P('fsdp')
- steps_next: int32 [16], replicated
- outputs: bfloat16 [512, 5120], P('dp', 'fsdp')
All inputs are finite; a program needn't handle non-finite values. No bound on the sum of `flags` on one device may be relied on, other than what follows from the above.
Results may differ from a plain program's by a relative error of at most 0.0049.
Values may be sent and summed in bfloat16 or wider, within the bound.
A program may use at most 128 MiB of HBM per device.

v0:
```python
import jax
import jax.numpy as jnp
from jax import lax
from jax.sharding import PartitionSpec as P

BUCKETS = 16
first_decay = 0.9
second_decay = 0.95
epsilon = 1e-08


def local(tokens, out_grad, master, moment_one, moment_two, flags, steps, rate):
    width_out = master.shape[1]
    bucket_width = width_out // BUCKETS
    contract_rows = (((0,), (0,)), ((), ()))
    rows = lax.all_gather(tokens, "dp", axis=0, tiled=True)
    grads = lax.all_gather(
        lax.all_gather(out_grad, "fsdp", axis=1, tiled=True), "dp", axis=0, tiled=True
    )
    counts = lax.psum(flags[0], ("fsdp", "dp"))
    gradient = lax.dot_general(rows, grads, contract_rows, preferred_element_type=jnp.float32)
    commit_bucket = counts == 0
    commit = jnp.repeat(commit_bucket, bucket_width)[None, :]
    times = jnp.repeat(steps + 1, bucket_width).astype(jnp.float32)[None, :]
    first = first_decay * moment_one + (1.0 - first_decay) * gradient
    second = second_decay * moment_two + (1.0 - second_decay) * gradient * gradient
    fix_one = 1.0 - jnp.power(jnp.float32(first_decay), times)
    fix_two = 1.0 - jnp.power(jnp.float32(second_decay), times)
    candidate = master - rate[0] * (first / fix_one) / (jnp.sqrt(second / fix_two) + epsilon)
    master_next = jnp.where(commit, candidate, master)
    moment_one_next = jnp.where(commit, first, moment_one)
    moment_two_next = jnp.where(commit, second, moment_two)
    weight_half = master_next.astype(jnp.bfloat16)
    steps_next = steps + commit_bucket.astype(jnp.int32)
    share = lax.dot_general(
        tokens, weight_half, (((1,), (0,)), ((), ())), preferred_element_type=jnp.float32
    ).astype(jnp.bfloat16)
    shards = lax.axis_size("fsdp")
    pieces = share.reshape(share.shape[0], shards, -1).transpose(1, 0, 2)
    result = jnp.sum(lax.all_to_all(pieces, "fsdp", 0, 0).astype(jnp.float32), axis=0)
    return (
        master_next,
        moment_one_next,
        moment_two_next,
        weight_half,
        steps_next,
        result.astype(jnp.bfloat16),
    )


def solution(mesh):
    in_specs = (
        P("dp", "fsdp"),
        P("dp", "fsdp"),
        P("fsdp", None),
        P("fsdp", None),
        P("fsdp", None),
        P(("fsdp", "dp"), None),
        P(),
        P(),
    )
    out_specs = (
        P("fsdp", None),
        P("fsdp", None),
        P("fsdp", None),
        P("fsdp", None),
        P(),
        P("dp", "fsdp"),
    )
    return jax.shard_map(local, mesh=mesh, in_specs=in_specs, out_specs=out_specs, check_vma=False)
```

profile of v0, /device:TPU:0, one launch (start us, length us, event | category | flops | bytes accessed | tf_op | source)
XLA Modules:
  0.0 180.5 jit_solution(914096782585376441)
XLA Ops:
  7.2 0.0 all-gather.3.cloned.1.call-start
  7.2 0.7 all-gather.3.cloned.1.call-update
  7.9 0.0 all-gather.5.cloned.1.call-start
  7.9 47.6 %all-gather.3.cloned.1.call-done = bf16[128,5120]{1,0:T(8,128)(2,1)} async-done(((bf16[128,640]{1,0:T(8,128)(2,1)}), bf16[128,5120]{1,0:T(8,128)(2,1)}) %all-gather.3.cloned.1.call-update) | async-done | bytes 1310736 | tf_op jit(solution)/shard_map/all_gather | solution.py:18
  55.5 0.0 all-gather.5.cloned.1.call-update
  55.5 39.6 %psum.7 = s32[16]{0:T(128)S(1)} all-reduce(s32[16]{0:T(128)} %bitcast.12), channel_id=1, replica_groups=mesh['fsdp'=8,'dp'=4] {'fsdp','dp'}, use_global_device_ids=true, to_apply=%region_0.0 | all-reduce | flops 16 | bytes 128 | tf_op jit(solution)/shard_map/psum | solution.py:20
  95.9 0.1 broadcast_in_dim.25
  95.9 0.1 broadcast_in_dim.26
  96.0 0.7 power_subtract_fusion.1
  96.7 0.1 broadcast_in_dim.28
  96.8 0.1 sub.28
  96.8 0.1 broadcast_in_dim.29
  96.9 0.1 sub.30
  97.0 8.2 %all_gather.9 = bf16[512,512]{1,0:T(8,128)(2,1)S(1)} all-gather(bf16[128,512]{1,0:T(8,128)(2,1)} %param.8), channel_id=1, replica_groups=mesh['fsdp'=8,'dp'=4] {'dp'}, dimensions={0}, use_global_device_ids=true | all-gather | bytes 655360 | tf_op jit(solution)/shard_map/all_gather | solution.py:16
  105.2 0.0 all-gather.5.cloned.1.call-done
  105.2 26.5 %fusion.3 = (bf16[512,5120]{1,0:T(8,128)(2,1)}, f32[512,5120]{1,0:T(8,128)}, f32[512,5120]{1,0:T(8,128)}, f32[512,5120]{1,0:T(8,128)}) fusion(f32[512,5120]{1,0:T(8,128)} %param.10, f32[5120]{0:T(1024)S(1)} %sub.30, f32[512,5120]{1,0:T(8,128)} %param.12, f32[5120]{0:T(1024)S(1)} %sub.28, f32[512,5120]{1,0:T(8,128)} %param.11, f32[]{:T(128)} %bitcast.11, ...), kind=kOutput, calls=%fused_computation.11 | convolution fusion | flops 2728919040 | bytes 73970688 | tf_op jit(solution)/shard_map/dot_general | solution.py:21
  131.7 0.0 copy-done
  131.7 5.2 %convolution_convert_fusion = bf16[5120,128]{1,0:T(8,128)(2,1)} fusion(bf16[512,5120]{1,0:T(8,128)(2,1)} %get-tuple-element.12, bf16[128,512]{1,0:T(8,128)(2,1)S(1)} %copy-done), kind=kOutput, calls=%fused_computation.6 | convolution fusion | flops 671744000 | bytes 6684672 | tf_op jit(solution)/shard_map/dot_general | solution.py:35
  136.8 3.9 %all-to-all-start = ((bf16[8,128,640]{1,2,0:T(8,128)(2,1)}), bf16[8,128,640]{1,2,0:T(8,128)(2,1)S(1)}, u32[]{:S(2)}, u32[]{:S(2)}) async-start(bf16[8,128,640]{1,2,0:T(8,128)(2,1)} %bitcast.4), calls=%async_computation | async-start | bytes 2621440 | tf_op jit(solution)/shard_map/all_to_all | solution.py:40
  140.7 0.0 copy-done.1
  140.7 0.5 convert_add_fusion
  141.2 31.4 %all-to-all-done = bf16[8,128,640]{1,2,0:T(8,128)(2,1)S(1)} async-done(((bf16[8,128,640]{1,2,0:T(8,128)(2,1)}), bf16[8,128,640]{1,2,0:T(8,128)(2,1)S(1)}, u32[]{:S(2)}, u32[]{:S(2)}) %all-to-all-start) | async-done | bytes 1310752 | tf_op jit(solution)/shard_map/all_to_all | solution.py:40
  172.6 0.2 reduce_sum.12
  172.8 0.8 copy.14
  (3 shorter events, 0.0 us)
Async XLA Ops:
  7.2 48.3 %all-gather.3.cloned.1.call-start = ((), (), s32[]{:S(2)}) async-start(), calls=%async_computation.1 | async-start | bytes 1474560 | tf_op jit(solution)/shard_map/all_gather | solution.py:18
  7.9 97.3 %all-gather.5.cloned.1.call-start = ((), (), s32[]{:S(2)}) async-start(), calls=%async_computation.2 | async-start | bytes 6553600 | tf_op jit(solution)/shard_map/all_gather | solution.py:17
  105.2 26.5 %copy-start = (bf16[128,512]{1,0:T(8,128)(2,1)S(1)}, bf16[128,512]{1,0:T(8,128)(2,1)}, u32[]{:S(2)}) copy-start(bf16[128,512]{1,0:T(8,128)(2,1)} %param.8) | copy-start | bytes 393220
  105.2 35.6 %copy-start.1 = (s32[16]{0:T(128)S(1)}, s32[16]{0:T(128)}, u32[]{:S(2)}) copy-start(s32[16]{0:T(128)} %param.14) | copy-start | bytes 196
  136.8 35.8 %all-to-all-start = ((bf16[8,128,640]{1,2,0:T(8,128)(2,1)}), bf16[8,128,640]{1,2,0:T(8,128)(2,1)S(1)}, u32[]{:S(2)}, u32[]{:S(2)}) async-start(bf16[8,128,640]{1,2,0:T(8,128)(2,1)} %bitcast.4), calls=%async_computation | async-start | bytes 2621440 | tf_op jit(solution)/shard_map/all_to_all | solution.py:40
Sparse Core Ops, SparseCore 0:
  10.2 45.2 all-gather.2
  57.1 39.8 all-gather.4
where the time goes:
time: 181 us; the launch traced here: 180 us
  waiting for transfers between devices  79.6 us (44%)
  blocking collectives  47.8 us (26%)
  matrix products  31.7 us (18%)
  between operations  14.7 us (8%)
  starting transfers between devices  3.94 us (2%)
    all_gather x1, waiting for transfers between devices, local(): lax.all_gather(out_grad, 'fsdp', axis=1, tiled=True)  47.6 us
    psum x1, blocking collectives, local(): counts = lax.psum(flags[0], ('fsdp', 'dp'))  39.6 us
    all_to_all x1, waiting for transfers between devices, local(): lax.all_to_all(pieces, 'fsdp', 0, 0).astype(jnp.float32)  31.4 us
    dot_general x1, matrix products, local(): lax.dot_general(rows, grads, contract_rows, preferred_element_type=jnp.fl...  26.5 us
    all_gather x1, blocking collectives, local(): rows = lax.all_gather(tokens, 'dp', axis=0, tiled=True)  8.16 us
    dot_general x1, matrix products, local(): lax.dot_general(tokens, weight_half, (((1,), (0,)), ((), ())), preferred_...  5.16 us
    all_to_all x1, starting transfers between devices, local(): lax.all_to_all(pieces, 'fsdp', 0, 0).astype(jnp.float32)  3.87 us
  transfers between devices with their start and end apart: 3, of which 2 were waited for; matrix products, arithmetic and copies ran while one was open for 1% of the time, Pallas kernels for 0%

commit v1 on v0

--- a/solution.py
+++ b/solution.py
@@ -15,7 +15,12 @@
     contract_rows = (((0,), (0,)), ((), ()))
     rows = lax.all_gather(tokens, "dp", axis=0, tiled=True)
     grads = lax.all_gather(
-        lax.all_gather(out_grad, "fsdp", axis=1, tiled=True), "dp", axis=0, tiled=True
+        jnp.concatenate(
+            lax.all_to_all(jnp.stack([out_grad] * lax.axis_size("fsdp")), "fsdp", 0, 0), axis=1
+        ),
+        "dp",
+        axis=0,
+        tiled=True,
     )
     counts = lax.psum(flags[0], ("fsdp", "dp"))
     gradient = lax.dot_general(rows, grads, contract_rows, preferred_element_type=jnp.float32)

time: 181 us -> 172 us (0.950)
  waiting for transfers between devices: 79.6 us -> 31.4 us
  blocking collectives: 47.8 us -> 86.6 us
    all_gather x2 -> x1, waiting for transfers between devices: 47.6 us -> 0.01 us  [local(): lax.all_gather(jnp.concatenate(lax.all_to_all(jnp.stack([out_grad] * lax....]
    all_to_all x0 -> x1, blocking collectives: none -> 38.6 us  [local(): lax.all_to_all(jnp.stack([out_grad] * lax.axis_size('fsdp')), 'fsdp', 0, 0)]
  transfers between devices with their start and end apart: 3 -> 2, of which waited for: 2 -> 1; matrix products, arithmetic and copies ran while one was open for 1% -> 1% of each run, Pallas kernels for 0% -> 0%
where the time goes in v1:
time: 172 us
  blocking collectives  86.6 us (50%)
  waiting for transfers between devices  31.4 us (18%)
  matrix products  31.4 us (18%)
  between operations  14.7 us (9%)
  starting transfers between devices  3.85 us (2%)
  local copies, waits for them, and re-layouts  2.54 us (1%)
    psum x1, blocking collectives, local(): counts = lax.psum(flags[0], ('fsdp', 'dp'))  39.8 us
    all_to_all x1, blocking collectives, local(): lax.all_to_all(jnp.stack([out_grad] * lax.axis_size('fsdp')), 'fsdp', 0, 0)  38.6 us
    all_to_all x1, waiting for transfers between devices, local(): lax.all_to_all(pieces, 'fsdp', 0, 0).astype(jnp.float32)  31.4 us
    dot_general x1, matrix products, local(): lax.dot_general(rows, grads, contract_rows, preferred_element_type=jnp.fl...  26.3 us
    all_gather x1, blocking collectives, local(): rows = lax.all_gather(tokens, 'dp', axis=0, tiled=True)  8.16 us
    dot_general x1, matrix products, local(): lax.dot_general(tokens, weight_half, (((1,), (0,)), ((), ())), preferred_...  5.13 us
    all_to_all x1, starting transfers between devices, local(): lax.all_to_all(pieces, 'fsdp', 0, 0).astype(jnp.float32)  3.81 us
  transfers between devices with their start and end apart: 2, of which 1 were waited for; matrix products, arithmetic and copies ran while one was open for 1% of the time, Pallas kernels for 0%

profile of v1, /device:TPU:0, one launch (start us, length us, event | category | flops | bytes accessed | tf_op | source)
XLA Modules:
  0.0 171.9 jit_solution(1600665184070423364)
XLA Ops:
  7.2 0.0 all-gather.2.cloned.1.call-start
  7.2 1.1 copy.15
  8.3 0.2 stack.2
  8.5 38.6 %all_to_all.10 = bf16[8,128,640]{1,2,0:T(8,128)(2,1)} all-to-all(bf16[8,128,640]{1,2,0:T(8,128)(2,1)S(1)} %stack.2), channel_id=1, replica_groups=mesh['fsdp'=8,'dp'=4] {'fsdp'}, dimensions={0} | all-to-all | bytes 2621440 | tf_op jit(solution)/shard_map/all_to_all | solution.py:19
  47.1 0.0 all-gather.2.cloned.1.call-update
  47.1 39.8 %psum.7 = s32[16]{0:T(128)S(1)} all-reduce(s32[16]{0:T(128)} %bitcast.16), channel_id=1, replica_groups=mesh['fsdp'=8,'dp'=4] {'fsdp','dp'}, use_global_device_ids=true, to_apply=%region_0.0 | all-reduce | flops 16 | bytes 128 | tf_op jit(solution)/shard_map/psum | solution.py:25
  87.6 0.1 broadcast_in_dim.25
  87.7 0.1 broadcast_in_dim.26
  87.8 0.7 power_subtract_fusion.1
  88.4 0.1 broadcast_in_dim.28
  88.5 0.1 sub.28
  88.6 0.1 broadcast_in_dim.29
  88.7 0.1 sub.30
  88.7 8.2 %all_gather.6 = bf16[512,512]{1,0:T(8,128)(2,1)S(1)} all-gather(bf16[128,512]{1,0:T(8,128)(2,1)} %param.8), channel_id=1, replica_groups=mesh['fsdp'=8,'dp'=4] {'dp'}, dimensions={0}, use_global_device_ids=true | all-gather | bytes 655360 | tf_op jit(solution)/shard_map/all_gather | solution.py:16
  96.9 0.0 all-gather.2.cloned.1.call-done
  96.9 26.3 %fusion.3 = (bf16[512,5120]{1,0:T(8,128)(2,1)}, f32[512,5120]{1,0:T(8,128)}, f32[512,5120]{1,0:T(8,128)}, f32[512,5120]{1,0:T(8,128)}) fusion(f32[512,5120]{1,0:T(8,128)} %param.10, f32[5120]{0:T(1024)S(1)} %sub.30, f32[512,5120]{1,0:T(8,128)} %param.12, f32[5120]{0:T(1024)S(1)} %sub.28, f32[512,5120]{1,0:T(8,128)} %param.11, f32[]{:T(128)} %bitcast.14, ...), kind=kOutput, calls=%fused_computation.11 | convolution fusion | flops 2728919040 | bytes 73970688 | tf_op jit(solution)/shard_map/dot_general | solution.py:26
  123.2 0.0 copy-done
  123.2 5.1 %convolution_convert_fusion = bf16[5120,128]{1,0:T(8,128)(2,1)} fusion(bf16[512,5120]{1,0:T(8,128)(2,1)} %get-tuple-element.12, bf16[128,512]{1,0:T(8,128)(2,1)S(1)} %copy-done), kind=kOutput, calls=%fused_computation.6 | convolution fusion | flops 671744000 | bytes 6684672 | tf_op jit(solution)/shard_map/dot_general | solution.py:40
  128.3 3.8 %all-to-all-start.1 = ((bf16[8,128,640]{1,2,0:T(8,128)(2,1)}), bf16[8,128,640]{1,2,0:T(8,128)(2,1)S(1)}, u32[]{:S(2)}, u32[]{:S(2)}) async-start(bf16[8,128,640]{1,2,0:T(8,128)(2,1)} %bitcast.6), calls=%async_computation.1 | async-start | bytes 2621440 | tf_op jit(solution)/shard_map/all_to_all | solution.py:45
  132.1 0.0 copy-done.1
  132.1 0.5 convert_add_fusion
  132.6 31.4 %all-to-all-done.1 = bf16[8,128,640]{1,2,0:T(8,128)(2,1)S(1)} async-done(((bf16[8,128,640]{1,2,0:T(8,128)(2,1)}), bf16[8,128,640]{1,2,0:T(8,128)(2,1)S(1)}, u32[]{:S(2)}, u32[]{:S(2)}) %all-to-all-start.1) | async-done | bytes 1310752 | tf_op jit(solution)/shard_map/all_to_all | solution.py:45
  164.0 0.2 reduce_sum.12
  164.2 0.8 copy.16
  (3 shorter events, 0.0 us)
Async XLA Ops:
  7.2 89.7 %all-gather.2.cloned.1.call-start = ((), (), s32[]{:S(2)}) async-start(), calls=%async_computation.2 | async-start | bytes 6553600 | tf_op jit(solution)/shard_map/all_gather | solution.py:17
  96.9 26.3 %copy-start = (bf16[128,512]{1,0:T(8,128)(2,1)S(1)}, bf16[128,512]{1,0:T(8,128)(2,1)}, u32[]{:S(2)}) copy-start(bf16[128,512]{1,0:T(8,128)(2,1)} %param.8) | copy-start | bytes 393220
  96.9 35.2 %copy-start.1 = (s32[16]{0:T(128)S(1)}, s32[16]{0:T(128)}, u32[]{:S(2)}) copy-start(s32[16]{0:T(128)} %param.14) | copy-start | bytes 196
  128.3 35.7 %all-to-all-start.1 = ((bf16[8,128,640]{1,2,0:T(8,128)(2,1)}), bf16[8,128,640]{1,2,0:T(8,128)(2,1)S(1)}, u32[]{:S(2)}, u32[]{:S(2)}) async-start(bf16[8,128,640]{1,2,0:T(8,128)(2,1)} %bitcast.6), calls=%async_computation.1 | async-start | bytes 2621440 | tf_op jit(solution)/shard_map/all_to_all | solution.py:45
Sparse Core Ops, SparseCore 0:
  47.2 40.7 all-gather.1
